TPU v7x, 128 devices: a whole 4x4x4 slice. The times are simulated.
128 devices in a mesh: table: 32 (over x, y, core), batch: 4 (over z).
Axes of the slice: x: 4, y: 4, z: 4, core: 2. Of those that a mesh axis runs over, the one named last changes fastest.
Arguments:
- queries: bfloat16 [512, 4, 512], P(('table', 'batch')), may hold values from -5 to 5
- indices: int32 [512, 4, 32], P(('table', 'batch')), may hold values from 0 to 1048575, as said below
- first_keys: bfloat16 [4, 1024, 256], P(None, ('table', 'batch')), may hold values from -4 to 4
- second_keys: bfloat16 [4, 1024, 256], replicated, may hold values from -4 to 4
- values: bfloat16 [1048576, 1024], P(('table', 'batch')), may hold values from -6 to 6
Outputs:
- memory_read: bfloat16 [512, 1024], P(('table', 'batch'))
Inputs may be any that keep to these rules, and one draw needn't show every extreme that they name: `indices`: row r of the value table belongs to device r // 8192 of table+batch. The entries of the 4 sequences of one device name rows of any one owner at most 8 times, and one owner is named exactly 8 times by the entries of every device.
All inputs are finite; a program needn't handle non-finite values.
Results may differ from a plain program's by a relative error of at most 0.005.
Values may be sent and summed in bfloat16 or wider, within the bound.
No kernel may reach another device: no remote copies, remote signals or barrier semaphores. Data moves between devices by JAX's collectives and lax.ppermute only.
A program may use at most 64 MiB of HBM per device.

v0:
```python
import jax
import jax.numpy as jnp
from jax import lax
from jax.sharding import PartitionSpec as P


def decode_codes(codes, head_count, table_rows):
    usable = codes >= 0
    local_row = jnp.where(usable, codes % table_rows, -1)
    head_ids = jnp.where(usable, codes // table_rows % head_count, 0)
    seq_local = jnp.where(usable, codes // (table_rows * head_count), -1)
    return (usable, local_row, head_ids, seq_local)


def answer_slots(request_pair, first_keys, values):
    query_first, codes = request_pair
    head_count, first_count, half_width = first_keys.shape
    table_rows = values.shape[0]
    sub_count = table_rows // first_count
    usable, local_row, head_ids, seq_local = decode_codes(codes, head_count, table_rows)
    key_slot = jnp.where(usable, head_ids * first_count + local_row // sub_count, -1)
    key_pick = (
        key_slot[..., None] == jnp.arange(head_count * first_count, dtype=jnp.int32)
    ).astype(jnp.bfloat16)
    key_rows = jnp.einsum(
        "dnc,ck->dnk",
        key_pick,
        first_keys.reshape(head_count * first_count, half_width),
        preferred_element_type=jnp.float32,
    )
    first_part = jnp.sum(query_first.astype(jnp.float32) * key_rows, axis=-1)
    row_pick = (local_row[..., None] == jnp.arange(table_rows, dtype=jnp.int32)).astype(
        jnp.bfloat16
    )
    fetched = jnp.einsum(
        "dnv,vc->dnc", row_pick, values, preferred_element_type=jnp.float32
    ).astype(jnp.bfloat16)
    return (first_part, fetched, seq_local)


def second_scores(query_second, head_ids, columns, second_keys):
    head_count, sub_count, half_width = second_keys.shape
    key_table = second_keys.reshape(head_count * sub_count, half_width)
    where_rows = jnp.clip(head_ids * sub_count + columns, 0, head_count * sub_count - 1)
    key_rows = jnp.take(key_table, where_rows, axis=0)
    return jnp.sum(query_second.astype(jnp.float32) * key_rows.astype(jnp.float32), axis=-1)


def shards(queries, indices, first_keys, second_keys, values):
    seqs_dev, head_count, top_count = indices.shape
    half_width = queries.shape[2] // 2
    table_rows, value_width = values.shape
    sub_count = second_keys.shape[1]
    devices = lax.axis_size(("table", "batch"))
    entries = seqs_dev * head_count * top_count
    slot_cap = max(2, 2 * entries // devices)
    positions = jnp.arange(entries, dtype=jnp.int32)
    entry_seq = positions // (head_count * top_count)
    entry_head = positions // top_count % head_count
    flat_index = indices.reshape(entries)
    row_owner = flat_index // table_rows
    local_row = flat_index % table_rows
    entry_codes = (entry_seq * head_count + entry_head) * table_rows + local_row
    owner_hot = (row_owner[:, None] == jnp.arange(devices, dtype=jnp.int32)[None, :]).astype(
        jnp.int32
    )
    slot_rank = jnp.sum(jnp.cumsum(owner_hot, axis=0) * owner_hot, axis=1) - 1
    slot_index = row_owner * slot_cap + slot_rank
    placed = slot_index[:, None] == jnp.arange(devices * slot_cap, dtype=jnp.int32)[None, :]
    query_entries = jnp.broadcast_to(
        queries[:, :, None, :], (seqs_dev, head_count, top_count, 2 * half_width)
    ).reshape(entries, 2 * half_width)
    query_slots = lax.dot_general(
        placed.astype(jnp.bfloat16),
        query_entries[:, :half_width],
        (((0,), (0,)), ((), ())),
        preferred_element_type=jnp.float32,
    )
    query_slots = query_slots.astype(jnp.bfloat16).reshape(devices, slot_cap, half_width)
    code_slots = (jnp.sum(jnp.where(placed, entry_codes[:, None] + 1, 0), axis=0) - 1).reshape(
        devices, slot_cap
    )
    first_slots, fetched, seq_local = answer_slots(
        (
            lax.all_to_all(
                query_slots, ("table", "batch"), split_axis=0, concat_axis=0, tiled=True
            ),
            lax.all_to_all(code_slots, ("table", "batch"), split_axis=0, concat_axis=0, tiled=True),
        ),
        first_keys,
        values,
    )
    returned = lax.all_to_all(
        first_slots, ("table", "batch"), split_axis=0, concat_axis=0, tiled=True
    ).reshape(devices * slot_cap)
    first_entries = jnp.sum(jnp.where(placed, returned[None, :], 0.0), axis=1)
    second_entries = second_scores(
        query_entries[:, half_width:], entry_head, flat_index % sub_count, second_keys
    )
    scores = (first_entries + second_entries).reshape(seqs_dev, head_count, top_count)
    best_score = jnp.max(scores, axis=-1, keepdims=True)
    raised = jnp.exp(scores - best_score)
    weights = (raised / jnp.sum(raised, axis=-1, keepdims=True)).astype(jnp.bfloat16)
    slot_weights = jnp.sum(
        jnp.where(placed, weights.reshape(entries).astype(jnp.float32)[:, None], 0.0), axis=0
    ).astype(jnp.bfloat16)
    rows_home = lax.all_to_all(
        fetched, ("table", "batch"), split_axis=0, concat_axis=0, tiled=True
    ).reshape(devices * slot_cap, value_width)
    slot_seqs = jnp.sum(jnp.where(placed, entry_seq[:, None] + 1, 0), axis=0) - 1
    mixing = jnp.where(
        jnp.arange(seqs_dev, dtype=jnp.int32)[:, None] == slot_seqs[None, :],
        slot_weights[None, :],
        jnp.zeros((), jnp.bfloat16),
    )
    output = jnp.dot(mixing, rows_home, preferred_element_type=jnp.float32)
    return output.astype(jnp.bfloat16)


def solution(mesh):
    placed = (
        P(("table", "batch"), None, None),
        P(("table", "batch"), None, None),
        P(None, ("table", "batch"), None),
        P(),
        P(("table", "batch"), None),
    )
    return jax.shard_map(
        shards, mesh=mesh, in_specs=placed, out_specs=P(("table", "batch"), None), check_vma=False
    )
```

profile of v0, /device:TPU:1, one launch (start us, length us, event | category | flops | bytes accessed | tf_op | source)
XLA Modules:
  0.0 118.3 jit_solution(6841943772395714837)
XLA Ops:
  0.0 0.0 copy-start
  0.0 0.9 reshape.416
  0.9 0.8 reshape.417
  1.7 0.1 copy.22
  1.9 0.2 fusion.19
  2.2 0.0 copy-start.2
  2.2 0.2 fusion.18
  2.4 0.5 select_reduce_fusion.3
  2.9 0.7 sub.68
  3.6 11.5 %all-to-all-start.1 = ((s32[128,1,8]{2,1,0:T(1,128)}), s32[128,1,8]{2,1,0:T(1,128)S(1)}, u32[]{:S(2)}, u32[]{:S(2)}) async-start(s32[128,1,8]{2,1,0:T(1,128)} %bitcast.5), calls=%async_computation.1 | async-start | bytes 131072 | tf_op jit(solution)/shard_map/all_to_all | solution.py:88
  15.1 0.8 broadcast_in_dim.92
  15.9 1.6 %fusion.12 = bf16[128,8,256]{2,1,0:T(8,128)(2,1)} fusion(s32[512]{0:T(512)S(1)} %add_add_fusion, bf16[512,512]{1,0:T(8,128)(2,1)S(1)} %bitcast.35), kind=kOutput, calls=%fused_computation.18 | convolution fusion | flops 269221888 | bytes 788480 | tf_op jit(solution)/shard_map/dot_general | solution.py:73
  17.5 7.3 %all-to-all-done.1 = s32[128,1,8]{2,1,0:T(1,128)S(1)} async-done(((s32[128,1,8]{2,1,0:T(1,128)}), s32[128,1,8]{2,1,0:T(1,128)S(1)}, u32[]{:S(2)}, u32[]{:S(2)}) %all-to-all-start.1) | async-done | bytes 4128 | tf_op jit(solution)/shard_map/all_to_all | solution.py:88
  24.8 4.3 %all-to-all-start = ((bf16[128,8,256]{2,1,0:T(8,128)(2,1)}), bf16[128,8,256]{2,1,0:T(8,128)(2,1)S(1)}, u32[]{:S(2)}, u32[]{:S(2)}) async-start(bf16[128,8,256]{2,1,0:T(8,128)(2,1)} %fusion.12), calls=%async_computation | async-start | bytes 1048576 | tf_op jit(solution)/shard_map/all_to_all | solution.py:85
  29.1 0.1 fusion.26
  29.3 0.1 copy.28
  29.4 13.7 %all-to-all-done = bf16[128,8,256]{2,1,0:T(8,128)(2,1)S(1)} async-done(((bf16[128,8,256]{2,1,0:T(8,128)(2,1)}), bf16[128,8,256]{2,1,0:T(8,128)(2,1)S(1)}, u32[]{:S(2)}, u32[]{:S(2)}) %all-to-all-start) | async-done | bytes 524320 | tf_op jit(solution)/shard_map/all_to_all | solution.py:85
  43.0 0.0 copy-done.2
  43.0 0.5 fusion.11
  43.5 0.7 copy.27
  44.2 4.1 %all-to-all-start.2 = ((f32[128,1,8]{2,1,0:T(1,128)}), f32[128,1,8]{2,1,0:T(1,128)S(1)}, u32[]{:S(2)}, u32[]{:S(2)}) async-start(f32[128,1,8]{2,1,0:T(1,128)} %copy.27), calls=%async_computation.2 | async-start | bytes 131072 | tf_op jit(solution)/shard_map/all_to_all | solution.py:93
  48.3 24.2 %fusion.7 = bf16[128,8,1024]{2,0,1:T(8,128)(2,1)S(1)} fusion(bf16[8192,1024]{1,0:T(8,128)(2,1)} %param.9, s32[128,8]{0,1:T(8,128)S(1)} %copy.28), kind=kOutput, calls=%fused_computation.14 | convolution fusion | flops 17189306368 | bytes 18878464 | tf_op jit(solution)/shard_map/dnv,vc->dnc/dot_general | solution.py:35
  72.5 2.5 %copy.29 = bf16[128,8,1024]{2,1,0:T(8,128)(2,1)} copy(bf16[128,8,1024]{2,0,1:T(8,128)(2,1)S(1)} %fusion.7) | data formatting | bytes 4194304 | tf_op jit(solution)/shard_map/convert_element_type | solution.py:37
  75.0 0.0 copy-start.1
  75.0 0.0 all-to-all-done.2
  75.0 10.2 %all-to-all-start.3 = ((bf16[128,8,1024]{2,1,0:T(8,128)(2,1)}), bf16[128,8,1024]{2,1,0:T(8,128)(2,1)}, u32[]{:S(2)}, u32[]{:S(2)}) async-start(bf16[128,8,1024]{2,1,0:T(8,128)(2,1)} %copy.29), calls=%async_computation.3 | async-start | bytes 4194304 | tf_op jit(solution)/shard_map/all_to_all | solution.py:107
  85.3 0.0 copy-done.1
  85.3 0.1 reshape.423
  85.4 0.0 copy-done
  85.4 2.0 %gather_fusion = bf16[512,256]{1,0:T(8,128)(2,1)S(1)} fusion(bf16[4096,256]{1,0:T(8,128)(2,1)S(1)} %bitcast.34, s32[1024]{0:T(1024)S(1)} %pad_clamp_fusion), kind=kCustom, calls=%fused_computation | custom fusion | bytes 526336 | tf_op jit(solution)/shard_map/jit(_take)/gather | solution.py:45
  87.4 0.2 multiply_reduce_fusion
  87.7 0.5 broadcast.638
  88.2 0.8 reduce.3
  89.0 0.1 broadcast_in_dim.94
  89.1 0.4 select_reduce_fusion.1
  89.4 0.1 add.237
  89.5 0.1 reduce_max.9
  89.6 0.2 fusion
  89.8 0.1 div.100
  89.9 0.1 sub.72
  89.9 0.1 sub.73
  90.0 0.3 select_reduce_fusion
  90.3 25.3 %all-to-all-done.3 = bf16[128,8,1024]{2,1,0:T(8,128)(2,1)} async-done(((bf16[128,8,1024]{2,1,0:T(8,128)(2,1)}), bf16[128,8,1024]{2,1,0:T(8,128)(2,1)}, u32[]{:S(2)}, u32[]{:S(2)}) %all-to-all-start.3) | async-done | bytes 2097184 | tf_op jit(solution)/shard_map/all_to_all | solution.py:107
  115.7 2.6 %fusion.13 = bf16[4,1024]{1,0:T(4,128)(2,1)} fusion(bf16[128,8,1024]{2,1,0:T(8,128)(2,1)} %all-to-all-done.3, s32[1024]{0:T(1024)S(1)} %broadcast_add_fusion.2, bf16[1024]{0:T(1024)(128)(2,1)S(1)} %select_reduce_fusion), kind=kOutput, calls=%fused_computation.19 | convolution fusion | flops 8400896 | bytes 2111488 | tf_op jit(solution)/shard_map/dot_general | solution.py:116
  (17 shorter events, 0.2 us)
Async XLA Ops:
  0.0 85.4 %copy-start = (bf16[4,1024,256]{2,1,0:T(8,128)(2,1)S(1)}, bf16[4,1024,256]{2,1,0:T(8,128)(2,1)}, u32[]{:S(2)}) copy-start(bf16[4,1024,256]{2,1,0:T(8,128)(2,1)} %param.8) | copy-start | bytes 6291460
  2.2 40.8 %copy-start.2 = (bf16[4,8,256]{2,1,0:T(8,128)(2,1)S(1)}, bf16[4,8,256]{2,1,0:T(8,128)(2,1)}, u32[]{:S(2)}) copy-start(bf16[4,8,256]{2,1,0:T(8,128)(2,1)} %param.7) | copy-start | bytes 49156
  3.6 21.2 %all-to-all-start.1 = ((s32[128,1,8]{2,1,0:T(1,128)}), s32[128,1,8]{2,1,0:T(1,128)S(1)}, u32[]{:S(2)}, u32[]{:S(2)}) async-start(s32[128,1,8]{2,1,0:T(1,128)} %bitcast.5), calls=%async_computation.1 | async-start | bytes 131072 | tf_op jit(solution)/shard_map/all_to_all | solution.py:88
  24.8 18.2 %all-to-all-start = ((bf16[128,8,256]{2,1,0:T(8,128)(2,1)}), bf16[128,8,256]{2,1,0:T(8,128)(2,1)S(1)}, u32[]{:S(2)}, u32[]{:S(2)}) async-start(bf16[128,8,256]{2,1,0:T(8,128)(2,1)} %fusion.12), calls=%async_computation | async-start | bytes 1048576 | tf_op jit(solution)/shard_map/all_to_all | solution.py:85
  44.2 30.8 %all-to-all-start.2 = ((f32[128,1,8]{2,1,0:T(1,128)}), f32[128,1,8]{2,1,0:T(1,128)S(1)}, u32[]{:S(2)}, u32[]{:S(2)}) async-start(f32[128,1,8]{2,1,0:T(1,128)} %copy.27), calls=%async_computation.2 | async-start | bytes 131072 | tf_op jit(solution)/shard_map/all_to_all | solution.py:93
  75.0 10.2 %copy-start.1 = (s32[4,4,32]{2,1,0:T(4,128)S(1)}, s32[4,4,32]{2,1,0:T(4,128)}, u32[]{:S(2)}) copy-start(s32[4,4,32]{2,1,0:T(4,128)} %param.6) | copy-start | bytes 6148
  75.0 40.6 %all-to-all-start.3 = ((bf16[128,8,1024]{2,1,0:T(8,128)(2,1)}), bf16[128,8,1024]{2,1,0:T(8,128)(2,1)}, u32[]{:S(2)}, u32[]{:S(2)}) async-start(bf16[128,8,1024]{2,1,0:T(8,128)(2,1)} %copy.29), calls=%async_computation.3 | async-start | bytes 4194304 | tf_op jit(solution)/shard_map/all_to_all | solution.py:107
where the time goes:
time: 119 us; the launch traced here: 118 us
  waiting for transfers between devices  46.3 us (39%)
  starting transfers between devices  30.1 us (25%)
  matrix products  28.8 us (24%)
  local copies, waits for them, and re-layouts  9.64 us (8%)
  other arithmetic  3.15 us (3%)
    all_to_all x1, waiting for transfers between devices, shards(): lax.all_to_all(fetched, ('table', 'batch'), split_axis=0, concat_axis=0,...  25.3 us
    dot_general x1, matrix products, answer_slots(): jnp.einsum('dnv,vc->dnc', row_pick, values, preferred_element_type=jnp.fl...  24.2 us
    all_to_all x1, waiting for transfers between devices, shards(): lax.all_to_all(query_slots, ('table', 'batch'), split_axis=0, concat_axis...  13.7 us
    all_to_all x1, starting transfers between devices, shards(): lax.all_to_all(code_slots, ('table', 'batch'), split_axis=0, concat_axis=...  11.5 us
    all_to_all x1, starting transfers between devices, shards(): lax.all_to_all(fetched, ('table', 'batch'), split_axis=0, concat_axis=0,...  10.2 us
    all_to_all x1, waiting for transfers between devices, shards(): lax.all_to_all(code_slots, ('table', 'batch'), split_axis=0, concat_axis=...  7.34 us
    all_to_all x1, starting transfers between devices, shards(): lax.all_to_all(query_slots, ('table', 'batch'), split_axis=0, concat_axis...  4.26 us
    all_to_all x1, starting transfers between devices, shards(): lax.all_to_all(first_slots, ('table', 'batch'), split_axis=0, concat_axis...  4.13 us
  transfers between devices with their start and end apart: 4, of which 3 were waited for; matrix products, arithmetic and copies ran while one was open for 29% of the time, Pallas kernels for 0%

commit v1 on v0

v1 whole, which is shorter than its diff:
```python
import jax
import jax.numpy as jnp
from jax import lax
from jax.experimental import pallas as pl
from jax.experimental.pallas import tpu as pltpu
from jax.sharding import Mesh, PartitionSpec as P

DEVICE_AXES = ("x", "y", "core", "z")
CHIP_AXES = ("x", "y", "z")
OWNER_AXES = ("core", "x", "y", "z")

SEQS = 4
HEADS = 4
TOPK = 32
GROUPS = SEQS * HEADS
ENTRIES = GROUPS * TOPK
HALF = 256
SUBS = 1024
KEYS_DEV = 8
CHIPS = 64
DEVICES = 128
VALS_DEV = 8192
DV = 1024
CAP = 8
LANES = 128
MIB = 1024 * 1024
ROW_LANE = 64
TILE = 8
NT = (((1,), (1,)), ((), ()))
NN = (((1,), (0,)), ((), ()))


def dot(a, b, dims):
    return lax.dot_general(a, b, dims, preferred_element_type=jnp.float32)


def iota(shape, axis):
    return lax.broadcasted_iota(jnp.int32, shape, axis)


def exchange(slots, axes):
    return lax.all_to_all(slots, axes, split_axis=0, concat_axis=0, tiled=True)


def picked(line, where):
    width = line.shape[1]
    total = jnp.zeros((TOPK, LANES), jnp.float32)
    for tile in range(width // LANES):
        lanes = iota((TOPK, LANES), 1) + tile * LANES
        part = jnp.broadcast_to(line[:, tile * LANES : (tile + 1) * LANES], (TOPK, LANES))
        total = total + jnp.where(lanes == where, part, 0.0)
    return jnp.sum(total, axis=1, keepdims=True)


def plan_kernel(
    core_ref, column_ref, line_ref, query_ref, keys_ref, second_ref, place_ref, rows_ref, lane_ref, owner_ref, scores
):
    core = core_ref[0]
    owners = line_ref[...] >> 13
    chips = ((owners >> 3) << 2) + (owners & 3)
    spots = ((owners >> 2) & 1) * CHIPS + chips
    owner_ref[...] = jnp.where(iota((DEVICES, ENTRIES), 0) == spots, 1.0, 0.0).astype(jnp.bfloat16)
    for head in range(HEADS):
        scores[head] = dot(query_ref[...], keys_ref[pl.ds(head * SUBS, SUBS), :], NT)
    for group in range(GROUPS):
        here = pl.ds(group * TOPK, TOPK)
        index = jnp.broadcast_to(column_ref[here, :], (TOPK, LANES))
        owner = index >> 13
        rank = jnp.zeros((TOPK, LANES), jnp.int32)
        for tile in range(ENTRIES // LANES):
            if tile * LANES > group * TOPK + TOPK - 1:
                continue
            other = jnp.broadcast_to(owners[:, tile * LANES : (tile + 1) * LANES], (TOPK, LANES))
            earlier = iota((TOPK, LANES), 1) + tile * LANES < iota((TOPK, LANES), 0) + group * TOPK
            rank = rank + jnp.where((other == owner) & earlier, 1, 0)
        rank = jnp.broadcast_to(
            jnp.sum(rank.astype(jnp.float32), axis=1, keepdims=True).astype(jnp.int32), (TOPK, LANES)
        )
        row = index & (VALS_DEV - 1)
        mark = row + 1
        lane = iota((TOPK, LANES), 1)
        slot_lane = lane == ROW_LANE + rank
        rows_ref[0, here, :] = jnp.where(slot_lane, (mark >> 6) << 6, 0).astype(jnp.float32).astype(jnp.bfloat16)
        rows_ref[1, here, :] = jnp.where(slot_lane, mark & 63, 0).astype(jnp.float32).astype(jnp.bfloat16)
        lane_ref[here, :] = (group // HEADS) * CAP + rank
        first = index >> 10
        chip = ((owner >> 3) << 2) + (owner & 3)
        away = jnp.where(((owner >> 2) & 1) == core, 0, 1)
        place_ref[here, :] = away * (CHIPS * KEYS_DEV) + chip * KEYS_DEV + (first & 7)
        line = scores[group % HEADS, pl.ds(group, 1), :]
        second_ref[here, :] = jnp.broadcast_to(picked(line, index & (SUBS - 1)), (TOPK, LANES))


def match_kernel(mine_ref, theirs_ref, keys_ref, mine_out, theirs_out):
    span = CHIPS * KEYS_DEV
    totals = [jnp.zeros((GROUPS, span), jnp.float32) for _ in range(2)]
    for head in range(HEADS):
        block = keys_ref[:, pl.ds(head * KEYS_DEV, KEYS_DEV), :].reshape(span, HALF)
        for side, ref in enumerate((mine_ref, theirs_ref)):
            found = dot(ref[...], block, NT)
            totals[side] = jnp.where(iota((GROUPS, span), 0) % HEADS == head, found, totals[side])
    mine_out[...] = totals[0]
    theirs_out[...] = totals[1]


def weigh_kernel(own_ref, away_ref, second_ref, place_ref, rows_ref, lane_ref, owner_ref, out_ref, weighed):
    span = CHIPS * KEYS_DEV
    for group in range(GROUPS):
        here = pl.ds(group * TOPK, TOPK)
        place = place_ref[here, :]
        line = pl.ds(group, 1)
        score = second_ref[here, :] + picked(own_ref[line, :], place) + picked(away_ref[line, :], place - span)
        raised = jnp.exp(score - jnp.max(score, axis=0, keepdims=True))
        weight = raised / jnp.sum(raised, axis=0, keepdims=True)
        hit = iota((TOPK, LANES), 1) == lane_ref[here, :]
        weighed[here, :] = jnp.where(hit, weight, 0.0).astype(jnp.bfloat16) + rows_ref[0, here, :]
    owner = owner_ref[...]
    total = dot(owner, weighed[...], NN) + dot(owner, rows_ref[1], NN)
    out_ref[:, 0, :] = total


def fetch_kernel(side_ref, mail_ref, values_ref, out_ref, row_words, row_spots, tiles, mixes, spot_sem, sems):
    blocks = 4
    side = side_ref[0]
    mail = mail_ref[pl.ds(side * CHIPS, CHIPS), 0, :]
    marks = mail.astype(jnp.int32)
    spare = iota((CHIPS, LANES), 0) * (CAP * TILE) + (iota((CHIPS, LANES), 1) & (CAP - 1)) * TILE
    rows = jnp.where(marks > 0, marks - 1, spare)
    row_words[...] = rows
    spots = pltpu.make_async_copy(row_words, row_spots, spot_sem)
    spots.start()
    spots.wait()
    chips_block = CHIPS // blocks
    rows_block = chips_block * CAP * TILE
    for block in range(blocks):

        def issue(step, carry, block=block):
            chip = block * chips_block + step
            for slot in range(CAP):
                row = row_spots[chip, ROW_LANE + slot]
                base = pl.multiple_of((row >> 3) << 3, TILE)
                spot = pl.multiple_of((chip * CAP + slot) * TILE, TILE)
                pltpu.make_async_copy(
                    values_ref.at[pl.ds(base, TILE)], tiles.at[pl.ds(spot, TILE)], sems.at[block]
                ).start()
            return carry

        lax.fori_loop(0, chips_block, issue, 0)
    spread = jnp.where(iota((8 * CHIPS, CHIPS), 0) >> 3 == iota((8 * CHIPS, CHIPS), 1), 1.0, 0.0)
    wide = dot(spread.astype(jnp.bfloat16), mail.astype(jnp.bfloat16), NN)
    mine = iota((8 * CHIPS, LANES), 1) >> 3 == iota((8 * CHIPS, LANES), 0) & 3
    wide = jnp.where(mine, wide, 0.0).astype(jnp.bfloat16)
    slot_of = (iota((LANES, rows_block), 1) >> 3) & (CAP - 1)
    slot_from = iota((LANES, rows_block), 0)
    copies = jnp.where(slot_from & (CAP - 1) == slot_of, 1.0, 0.0).astype(jnp.bfloat16)
    mixes[...] = dot(wide, copies, NN).astype(jnp.bfloat16)
    row_lanes = iota((CHIPS, LANES), 1) >> 3 == ROW_LANE >> 3
    within = jnp.where(row_lanes, rows & (TILE - 1), 0).astype(jnp.float32).astype(jnp.bfloat16)
    within = dot(within, jnp.where(slot_from == slot_of + ROW_LANE, 1.0, 0.0).astype(jnp.bfloat16), NN)
    outs_block = 8 * chips_block
    lane_chip = iota((chips_block, rows_block), 1) >> 6
    same = iota((outs_block, rows_block), 0) >> 3 == iota((outs_block, rows_block), 1) >> 6
    upper = iota((outs_block, DV // 2), 0) & 4 == 0
    for block in range(blocks):
        here = within[block * chips_block : (block + 1) * chips_block]
        here = jnp.where(iota((chips_block, rows_block), 0) == lane_chip, here, 0.0)
        here = jnp.sum(here, axis=0, keepdims=True).astype(jnp.int32)
        match = jnp.broadcast_to(here, (outs_block, rows_block)) == iota((outs_block, rows_block), 1) & (TILE - 1)
        mix = mixes[pl.ds(block * outs_block, outs_block), :].astype(jnp.float32)
        mix = jnp.where(same & match, mix, 0.0).astype(jnp.bfloat16)
        there = pl.ds(block * rows_block, rows_block)
        pltpu.make_async_copy(values_ref.at[pl.ds(0, rows_block)], tiles.at[there], sems.at[block]).wait()
        total = dot(mix, tiles[there, :], NN)
        out_ref[pl.ds(block * outs_block, outs_block), :] = jnp.where(
            upper, total[:, : DV // 2], total[:, DV // 2 :]
        ).astype(jnp.bfloat16)


def finish_kernel(parts_ref, out_ref):
    total = jnp.zeros((8, DV // 2), jnp.float32)
    for chip in range(CHIPS):
        total = total + parts_ref[chip].astype(jnp.float32)
    out_ref[:, : DV // 2] = total[:4].astype(jnp.bfloat16)
    out_ref[:, DV // 2 :] = total[4:].astype(jnp.bfloat16)


VMEM = pl.BlockSpec(memory_space=pltpu.VMEM)
SMEM = pl.BlockSpec(memory_space=pltpu.SMEM)
ANYWHERE = pl.BlockSpec(memory_space=pl.ANY)


def shaped(shape, dtype):
    return jax.ShapeDtypeStruct(shape, dtype)


def partial_rows(side, mail, values):
    return pl.pallas_call(
        fetch_kernel,
        out_shape=shaped((8 * CHIPS, DV // 2), jnp.bfloat16),
        in_specs=[SMEM, VMEM, ANYWHERE],
        out_specs=VMEM,
        scratch_shapes=[
            pltpu.VMEM((CHIPS, LANES), jnp.int32),
            pltpu.SMEM((CHIPS, LANES), jnp.int32),
            pltpu.VMEM((CAP * CHIPS * TILE, DV), jnp.bfloat16),
            pltpu.VMEM((8 * CHIPS, CAP * CHIPS * TILE // 4), jnp.bfloat16),
            pltpu.SemaphoreType.DMA,
            pltpu.SemaphoreType.DMA((4,)),
        ],
        compiler_params=pltpu.CompilerParams(vmem_limit_bytes=50 * MIB),
        cost_estimate=pl.CostEstimate(flops=10**9, bytes_accessed=3 * 1024 * 1024, transcendentals=0),
    )(side, mail, values)


def swapped(x):
    return lax.ppermute(x, "core", [(0, 1), (1, 0)])


def memory_read(queries, indices, first_keys, second_keys, values):
    core = lax.axis_index("core").astype(jnp.int32).reshape(1)
    keys = jnp.broadcast_to(
        first_keys.reshape(1, HEADS * KEYS_DEV, HALF), (CHIPS, HEADS * KEYS_DEV, HALF)
    )
    keys = exchange(keys, CHIP_AXES)
    asked = queries.reshape(GROUPS, 2 * HALF)
    asked_first = asked[:, :HALF]
    theirs = swapped(asked_first)

    plan = pl.pallas_call(
        plan_kernel,
        out_shape=(
            shaped((ENTRIES, LANES), jnp.float32),
            shaped((ENTRIES, LANES), jnp.int32),
            shaped((2, ENTRIES, LANES), jnp.bfloat16),
            shaped((ENTRIES, LANES), jnp.int32),
            shaped((DEVICES, ENTRIES), jnp.bfloat16),
        ),
        in_specs=[SMEM, VMEM, VMEM, VMEM, VMEM],
        out_specs=(VMEM,) * 5,
        scratch_shapes=[pltpu.VMEM((HEADS, GROUPS, SUBS), jnp.float32)],
        cost_estimate=pl.CostEstimate(flops=2 * 10**9, bytes_accessed=3 * 1024 * 1024, transcendentals=0),
        compiler_params=pltpu.CompilerParams(vmem_limit_bytes=12 * MIB),
        name="plan",
    )(
        core,
        indices.reshape(ENTRIES, 1),
        indices.reshape(1, ENTRIES),
        asked[:, HALF:],
        second_keys.reshape(HEADS * SUBS, HALF),
    )
    second, place, rows, lane, owner = plan

    span = CHIPS * KEYS_DEV
    own, away = pl.pallas_call(
        match_kernel,
        out_shape=(shaped((GROUPS, span), jnp.float32),) * 2,
        in_specs=[VMEM] * 3,
        out_specs=(VMEM,) * 2,
        compiler_params=pltpu.CompilerParams(vmem_limit_bytes=10 * MIB),
        name="match",
    )(asked_first, theirs, keys)
    away = swapped(away)
    mail = pl.pallas_call(
        weigh_kernel,
        out_shape=shaped((DEVICES, 1, LANES), jnp.float32),
        in_specs=[VMEM] * 7,
        out_specs=VMEM,
        scratch_shapes=[pltpu.VMEM((ENTRIES, LANES), jnp.bfloat16)],
        compiler_params=pltpu.CompilerParams(vmem_limit_bytes=8 * MIB),
        name="weigh",
    )(own, away, second, place, rows, lane, owner)
    mail = exchange(mail, OWNER_AXES)

    passed = swapped(partial_rows(1 - core, mail, values))
    kept = partial_rows(core, mail, values)
    both = (kept.astype(jnp.float32) + passed.astype(jnp.float32)).astype(jnp.bfloat16)
    parts = exchange(both.reshape(CHIPS, 8, DV // 2), CHIP_AXES)
    return pl.pallas_call(
        finish_kernel,
        out_shape=shaped((SEQS, DV), jnp.bfloat16),
        in_specs=[VMEM],
        out_specs=VMEM,
        compiler_params=pltpu.CompilerParams(vmem_limit_bytes=8 * MIB),
        name="finish",
    )(parts)


def solution(mesh):
    chips = Mesh(mesh.devices.reshape(4, 4, 2, 4), DEVICE_AXES)
    return jax.shard_map(
        memory_read,
        mesh=chips,
        in_specs=(
            P(DEVICE_AXES, None, None),
            P(DEVICE_AXES, None, None),
            P(None, DEVICE_AXES, None),
            P(),
            P(DEVICE_AXES, None),
        ),
        out_specs=P(DEVICE_AXES, None),
        check_vma=False,
    )
```

time: 119 us -> 83.1 us (0.70)
  matrix products: 28.8 us -> 0 us
  waiting for transfers between devices: 46.3 us -> 22.4 us
  blocking collectives: 0 us -> 17.1 us
  Pallas kernels: 0 us -> 16.2 us
  starting transfers between devices: 30.1 us -> 20.2 us
  local copies, waits for them, and re-layouts: 9.64 us -> 5.88 us
  other arithmetic: 3.15 us -> 0.14 us
    dot_general x4 -> x0, matrix products: 28.8 us -> none  [the longest x1 24.2 us: answer_slots(): jnp.einsum('dnv,vc->dnc', row_pick, values, preferred_element_type=jnp.fl...]
    all_to_all x4 -> x2, waiting for transfers between devices: 46.3 us -> 22.4 us  [exchange(): return lax.all_to_all(slots, axes, split_axis=0, concat_axis=0, tiled=True)]
    all_to_all x0 -> x1, blocking collectives: none -> 17.1 us  [exchange(): return lax.all_to_all(slots, axes, split_axis=0, concat_axis=0, tiled=True)]
    pallas_call x0 -> x6, Pallas kernels: none -> 16.2 us  [the longest x2 11.6 us: partial_rows(): pl.pallas_call(fetch_kernel, out_shape=shaped((8 * CHIPS, DV // 2), jnp.b...]
    all_to_all x4 -> x2, starting transfers between devices: 30.1 us -> 15.4 us  [exchange(): return lax.all_to_all(slots, axes, split_axis=0, concat_axis=0, tiled=True)]
    ppermute x0 -> x3, starting transfers between devices: none -> 4.77 us  [swapped(): return lax.ppermute(x, 'core', [(0, 1), (1, 0)])]
    convert_element_type x1 -> x0, local copies, waits for them, and re-layouts: 2.5 us -> none  [answer_slots(): fetched = jnp.einsum('dnv,vc->dnc', row_pick, values, preferred_element_t...]
    gather x1 -> x0, local copies, waits for them, and re-layouts: 1.95 us -> none  [second_scores(): key_rows = jnp.take(key_table, where_rows, axis=0)]
  transfers between devices with their start and end apart: 4 -> 5, of which waited for: 3 -> 2; matrix products, arithmetic and copies ran while one was open for 29% -> 3% of each run, Pallas kernels for 0% -> 10%
where the time goes in v1:
time: 83.1 us; the launch traced here: 82 us
  waiting for transfers between devices  22.4 us (27%)
  starting transfers between devices  20.2 us (24%)
  blocking collectives  17.1 us (21%)
  Pallas kernels  16.2 us (19%)
  local copies, waits for them, and re-layouts  5.88 us (7%)
    all_to_all x2, waiting for transfers between devices, exchange(): return lax.all_to_all(slots, axes, split_axis=0, concat_axis=0, tiled=True)  22.4 us
    all_to_all x1, blocking collectives, exchange(): return lax.all_to_all(slots, axes, split_axis=0, concat_axis=0, tiled=True)  17.1 us
    all_to_all x2, starting transfers between devices, exchange(): return lax.all_to_all(slots, axes, split_axis=0, concat_axis=0, tiled=True)  15.4 us
    pallas_call x2, Pallas kernels, partial_rows(): pl.pallas_call(fetch_kernel, out_shape=shaped((8 * CHIPS, DV // 2), jnp.b...  11.6 us
    ppermute x3, starting transfers between devices, swapped(): return lax.ppermute(x, 'core', [(0, 1), (1, 0)])  4.77 us
    pallas_call x1, Pallas kernels, memory_read(): pl.pallas_call(plan_kernel, out_shape=(shaped((ENTRIES, LANES), jnp.float...  2.06 us
    broadcast_in_dim x1, local copies, waits for them, and re-layouts, memory_read(): jnp.broadcast_to(first_keys.reshape(1, HEADS * KEYS_DEV, HALF), (CHIPS, H...  1.82 us
  transfers between devices with their start and end apart: 5, of which 2 were waited for; matrix products, arithmetic and copies ran while one was open for 3% of the time, Pallas kernels for 10%

profile of v1, /device:TPU:1, one launch (start us, length us, event | category | flops | bytes accessed | tf_op | source)
XLA Modules:
  0.0 82.0 jit_solution(3759937597476872465)
XLA Ops:
  0.0 1.8 %broadcast_in_dim.8 = bf16[64,32,256]{2,1,0:T(8,128)(2,1)} broadcast(bf16[32,256]{1,0:T(8,128)(2,1)} %bitcast.6), dimensions={1,2} | broadcast | bytes 1064960 | tf_op jit(solution)/shard_map/broadcast_in_dim | solution.py:221
  1.8 12.0 %all-to-all-start = ((bf16[64,32,256]{2,1,0:T(8,128)(2,1)}), bf16[64,32,256]{2,1,0:T(8,128)(2,1)S(1)}, u32[]{:S(2)}, u32[]{:S(2)}) async-start(bf16[64,32,256]{2,1,0:T(8,128)(2,1)} %broadcast_in_dim.8), calls=%async_computation | async-start | bytes 2097152 | tf_op jit(solution)/shard_map/all_to_all | solution.py:42
  13.8 0.7 reshape.21
  14.5 1.0 %collective-permute-start = (bf16[16,256]{1,0:T(8,128)(2,1)S(1)}, bf16[16,256]{1,0:T(8,128)(2,1)S(1)}, u32[]{:S(2)}, u32[]{:S(2)}) collective-permute-start(bf16[16,256]{1,0:T(8,128)(2,1)S(1)} %get-tuple-element.20.mine_ref), channel_id=1, source_target_pairs={{0,4},{4,0},{1,5},{5,1},{2,6},{6,2},{3,7},{7,3},{8,12},{12,8},{9,1... | collective-permute-start | bytes 24584 | tf_op jit(solution)/shard_map/ppermute | solution.py:216
  15.5 1.0 %reshape.26.column_ref = s32[512,1]{1,0:T(8,128)S(1)} reshape(s32[4,4,32]{2,1,0:T(4,128)} %param.6) | data formatting | bytes 4096 | tf_op jit(solution)/shard_map/reshape | solution.py:246
  16.5 0.8 reshape.23.line_ref
  17.3 0.0 collective-permute-done.theirs_ref
  17.3 13.1 %all-to-all-done.keys_ref = bf16[64,32,256]{2,1,0:T(8,128)(2,1)S(1)} async-done(((bf16[64,32,256]{2,1,0:T(8,128)(2,1)}), bf16[64,32,256]{2,1,0:T(8,128)(2,1)S(1)}, u32[]{:S(2)}, u32[]{:S(2)}) %all-to-all-start) | async-done | bytes 1048608 | tf_op jit(solution)/shard_map/all_to_all | solution.py:42
  30.4 0.6 match.1
  31.0 2.9 %collective-permute-start.1 = (f32[16,512]{1,0:T(8,128)S(1)}, f32[16,512]{1,0:T(8,128)S(1)}, u32[]{:S(2)}, u32[]{:S(2)}) collective-permute-start(f32[16,512]{1,0:T(8,128)S(1)} %get-tuple-element.13), channel_id=1, source_target_pairs={{0,4},{4,0},{1,5},{5,1},{2,6},{6,2},{3,7},{7,3},{8,12},{12,8},{9,1... | collective-permute-start | bytes 98312 | tf_op jit(solution)/shard_map/ppermute | solution.py:216
  33.9 0.0 copy-start
  33.9 1.6 %copy-done = bf16[4,1024,256]{2,1,0:T(8,128)(2,1)S(1)} copy-done((bf16[4,1024,256]{2,1,0:T(8,128)(2,1)S(1)}, bf16[4,1024,256]{2,1,0:T(8,128)(2,1)}, u32[]{:S(2)}) %copy-start) | copy-done | bytes 2097176
  35.5 2.1 %plan.1 = (f32[512,128]{1,0:T(8,128)S(1)}, s32[512,128]{1,0:T(8,128)S(1)}, bf16[2,512,128]{2,1,0:T(8,128)(2,1)S(1)}, s32[512,128]{1,0:T(8,128)S(1)}, bf16[128,512]{1,0:T(8,128)(2,1)S(1)}) custom-call(s32[1]{0:T(128)} %bitcast.core_ref.side_ref, s32[512,1]{1,0:T(8,128)S(1)} %reshape.26.column_ref, s32[1,512]{1,0:T(1,128)S(1)} %reshape.23.line_ref, ...), custom_call_target="tpu_custom_call" | custom-call | flops 2000000000 | bytes 3145728 | tf_op jit(solution)/shard_map/plan/pallas_call | solution.py:229
  37.6 0.0 collective-permute-done.1.away_ref
  37.6 1.2 %weigh.1 = f32[128,1,128]{2,1,0:T(1,128)} custom-call(f32[16,512]{1,0:T(8,128)S(1)} %get-tuple-element.12.own_ref, f32[16,512]{1,0:T(8,128)S(1)} %collective-permute-done.1.away_ref, f32[512,128]{1,0:T(8,128)S(1)} %get-tuple-element.14.second_ref, s32[512,128]{1,0:T(8,128)S(1)} %get-tuple-element.15.place_ref, ...), custom_call_target="tpu_custom_call" | custom-call | tf_op jit(solution)/shard_map/weigh/pallas_call | solution.py:263
  38.8 3.5 %all-to-all-start.1 = ((f32[128,1,128]{2,1,0:T(1,128)}), f32[128,1,128]{2,1,0:T(1,128)S(1)}, u32[]{:S(2)}, u32[]{:S(2)}) async-start(f32[128,1,128]{2,1,0:T(1,128)} %weigh.1), calls=%async_computation.1 | async-start | bytes 131072 | tf_op jit(solution)/shard_map/all_to_all | solution.py:42
  42.3 9.4 %all-to-all-done.1.mail_ref = f32[128,1,128]{2,1,0:T(1,128)S(1)} async-done(((f32[128,1,128]{2,1,0:T(1,128)}), f32[128,1,128]{2,1,0:T(1,128)S(1)}, u32[]{:S(2)}, u32[]{:S(2)}) %all-to-all-start.1) | async-done | bytes 65568 | tf_op jit(solution)/shard_map/all_to_all | solution.py:42
  51.7 5.8 %shard_map.56 = bf16[512,512]{1,0:T(8,128)(2,1)S(1)} custom-call(s32[1]{0:T(128)S(6)} %sub.3.side_ref, f32[128,1,128]{2,1,0:T(1,128)S(1)} %all-to-all-done.1.mail_ref, bf16[8192,1024]{1,0:T(8,128)(2,1)} %values_ref.3), custom_call_target="tpu_custom_call" | custom-call | flops 1000000000 | bytes 3145728 | tf_op jit(solution)/shard_map/pallas_call | solution.py:197
  57.5 0.8 collective-permute-start.2
  58.3 5.8 %shard_map.55 = bf16[512,512]{1,0:T(8,128)(2,1)S(1)} custom-call(s32[1]{0:T(128)} %bitcast.core_ref.side_ref, f32[128,1,128]{2,1,0:T(1,128)S(1)} %all-to-all-done.1.mail_ref, bf16[8192,1024]{1,0:T(8,128)(2,1)} %values_ref.3), custom_call_target="tpu_custom_call" | custom-call | flops 1000000000 | bytes 3145728 | tf_op jit(solution)/shard_map/pallas_call | solution.py:197
  64.1 0.0 collective-permute-done.2
  64.1 0.1 fusion
  64.3 17.1 %all_to_all.15.parts_ref = bf16[64,8,512]{2,1,0:T(8,128)(2,1)S(1)} all-to-all(bf16[64,8,512]{2,1,0:T(8,128)(2,1)S(1)} %fusion), channel_id=1, replica_groups=mesh['x'=4,'y'=4,'core'=2,'z'=4] {'x','y','z'}, dimensions={0} | all-to-all | bytes 1048576 | tf_op jit(solution)/shard_map/all_to_all | solution.py:42
  81.3 0.7 finish.1
  (1 shorter events, 0.0 us)
Async XLA Ops:
  1.8 28.5 %all-to-all-start = ((bf16[64,32,256]{2,1,0:T(8,128)(2,1)}), bf16[64,32,256]{2,1,0:T(8,128)(2,1)S(1)}, u32[]{:S(2)}, u32[]{:S(2)}) async-start(bf16[64,32,256]{2,1,0:T(8,128)(2,1)} %broadcast_in_dim.8), calls=%async_computation | async-start | bytes 2097152 | tf_op jit(solution)/shard_map/all_to_all | solution.py:42
  14.5 2.8 %collective-permute-start = (bf16[16,256]{1,0:T(8,128)(2,1)S(1)}, bf16[16,256]{1,0:T(8,128)(2,1)S(1)}, u32[]{:S(2)}, u32[]{:S(2)}) collective-permute-start(bf16[16,256]{1,0:T(8,128)(2,1)S(1)} %get-tuple-element.20.mine_ref), channel_id=1, source_target_pairs={{0,4},{4,0},{1,5},{5,1},{2,6},{6,2},{3,7},{7,3},{8,12},{12,8},{9,1... | collective-permute-start | bytes 24584 | tf_op jit(solution)/shard_map/ppermute | solution.py:216
  31.0 6.6 %collective-permute-start.1 = (f32[16,512]{1,0:T(8,128)S(1)}, f32[16,512]{1,0:T(8,128)S(1)}, u32[]{:S(2)}, u32[]{:S(2)}) collective-permute-start(f32[16,512]{1,0:T(8,128)S(1)} %get-tuple-element.13), channel_id=1, source_target_pairs={{0,4},{4,0},{1,5},{5,1},{2,6},{6,2},{3,7},{7,3},{8,12},{12,8},{9,1... | collective-permute-start | bytes 98312 | tf_op jit(solution)/shard_map/ppermute | solution.py:216
  33.9 1.6 %copy-start = (bf16[4,1024,256]{2,1,0:T(8,128)(2,1)S(1)}, bf16[4,1024,256]{2,1,0:T(8,128)(2,1)}, u32[]{:S(2)}) copy-start(bf16[4,1024,256]{2,1,0:T(8,128)(2,1)} %param.8) | copy-start | bytes 6291460
  38.8 12.9 %all-to-all-start.1 = ((f32[128,1,128]{2,1,0:T(1,128)}), f32[128,1,128]{2,1,0:T(1,128)S(1)}, u32[]{:S(2)}, u32[]{:S(2)}) async-start(f32[128,1,128]{2,1,0:T(1,128)} %weigh.1), calls=%async_computation.1 | async-start | bytes 131072 | tf_op jit(solution)/shard_map/all_to_all | solution.py:42
  57.5 6.6 %collective-permute-start.2 = (bf16[512,512]{1,0:T(8,128)(2,1)S(1)}, bf16[512,512]{1,0:T(8,128)(2,1)S(1)}, u32[]{:S(2)}, u32[]{:S(2)}) collective-permute-start(bf16[512,512]{1,0:T(8,128)(2,1)S(1)} %shard_map.56), channel_id=1, source_target_pairs={{0,4},{4,0},{1,5},{5,1},{2,6},{6,2},{3,7},{7,3},{8,12},{12,8},{9,1... | collective-permute-start | bytes 1572872 | tf_op jit(solution)/shard_map/ppermute | solution.py:216

commit v2 on v1

v2 whole, which is shorter than its diff:
```python
import jax
import jax.numpy as jnp
from jax import lax
from jax.experimental import pallas as pl
from jax.experimental.pallas import tpu as pltpu
from jax.sharding import Mesh, PartitionSpec as P

DEVICE_AXES = ("x", "y", "core", "half", "z")
CHIP_AXES = ("x", "y", "half", "z")
KEY_AXES = ("x", "y", "z")
OWNER_AXES = ("core", "x", "y", "half", "z")

SEQS = 4
HEADS = 4
TOPK = 32
GROUPS = SEQS * HEADS
ENTRIES = GROUPS * TOPK
HALF = 256
SUBS = 1024
KEYS_DEV = 8
CHIPS = 64
KEY_CHIPS = 32
QUARTER = KEY_CHIPS * KEYS_DEV
DEVICES = 128
VALS_DEV = 8192
DV = 1024
CAP = 8
LANES = 128
MIB = 1024 * 1024
ROW_LANE = 64
TILE = 8
AHEAD = 3
NT = (((1,), (1,)), ((), ()))
NN = (((1,), (0,)), ((), ()))


def dot(a, b, dims):
    return lax.dot_general(a, b, dims, preferred_element_type=jnp.float32)


def iota(shape, axis):
    return lax.broadcasted_iota(jnp.int32, shape, axis)


def exchange(slots, axes):
    return lax.all_to_all(slots, axes, split_axis=0, concat_axis=0, tiled=True)


def picked(line, where):
    width = line.shape[1]
    total = jnp.zeros((TOPK, LANES), jnp.float32)
    for tile in range(width // LANES):
        lanes = iota((TOPK, LANES), 1) + tile * LANES
        part = jnp.broadcast_to(line[:, tile * LANES : (tile + 1) * LANES], (TOPK, LANES))
        total = total + jnp.where(lanes == where, part, 0.0)
    return jnp.sum(total, axis=1, keepdims=True)


def repeat_kernel(keys_ref, out_ref):
    block = keys_ref[...]
    for chip in range(KEY_CHIPS):
        out_ref[chip] = block


def plan_kernel(
    here_ref,
    index_ref,
    query_ref,
    keys_ref,
    second_ref,
    place_ref,
    rows_ref,
    lane_ref,
    owner_ref,
    scores,
    keys,
    keys_sem,
):
    keys_copy = pltpu.make_async_copy(keys_ref, keys, keys_sem)
    keys_copy.start()
    flat = jnp.concatenate([index_ref[seq] for seq in range(SEQS)], axis=0)
    columns = flat.T
    owners = jnp.concatenate([flat[group : group + 1, :] for group in range(GROUPS)], axis=1) >> 13
    core = here_ref[0]
    half = here_ref[1]
    chips = ((owners >> 3) << 2) + (owners & 3)
    spots = ((owners >> 2) & 1) * CHIPS + chips
    owner_ref[...] = jnp.where(iota((DEVICES, ENTRIES), 0) == spots, 1.0, 0.0).astype(jnp.bfloat16)
    for group in range(GROUPS):
        here = pl.ds(group * TOPK, TOPK)
        index = jnp.broadcast_to(columns[:, group : group + 1], (TOPK, LANES))
        owner = index >> 13
        rank = jnp.zeros((TOPK, LANES), jnp.int32)
        for tile in range(ENTRIES // LANES):
            if tile * LANES > group * TOPK + TOPK - 1:
                continue
            other = jnp.broadcast_to(owners[:, tile * LANES : (tile + 1) * LANES], (TOPK, LANES))
            earlier = iota((TOPK, LANES), 1) + tile * LANES < iota((TOPK, LANES), 0) + group * TOPK
            rank = rank + jnp.where((other == owner) & earlier, 1, 0)
        rank = jnp.broadcast_to(
            jnp.sum(rank.astype(jnp.float32), axis=1, keepdims=True).astype(jnp.int32), (TOPK, LANES)
        )
        row = index & (VALS_DEV - 1)
        mark = row + 1
        lane = iota((TOPK, LANES), 1)
        slot_lane = lane == ROW_LANE + rank
        rows_ref[0, here, :] = jnp.where(slot_lane, (mark >> 6) << 6, 0).astype(jnp.float32).astype(jnp.bfloat16)
        rows_ref[1, here, :] = jnp.where(slot_lane, mark & 63, 0).astype(jnp.float32).astype(jnp.bfloat16)
        lane_ref[here, :] = (group // HEADS) * CAP + rank
        first = index >> 10
        chip = ((owner >> 3) << 1) + (owner & 1)
        away = jnp.where(((owner >> 2) & 1) == core, 0, 1) + jnp.where(((owner >> 1) & 1) == half, 0, 2)
        place_ref[here, :] = away * QUARTER + chip * KEYS_DEV + (first & 7)
    keys_copy.wait()
    for head in range(HEADS):
        scores[head] = dot(query_ref[...], keys[pl.ds(head * SUBS, SUBS), :], NT)
    for group in range(GROUPS):
        here = pl.ds(group * TOPK, TOPK)
        index = jnp.broadcast_to(columns[:, group : group + 1], (TOPK, LANES))
        line = scores[group % HEADS, pl.ds(group, 1), :]
        second_ref[here, :] = jnp.broadcast_to(picked(line, index & (SUBS - 1)), (TOPK, LANES))


def match_kernel(asked_0, asked_1, asked_2, asked_3, keys_ref, out_0, out_1, out_2, out_3):
    asked = jnp.concatenate([ref[...] for ref in (asked_0, asked_1, asked_2, asked_3)], axis=0)
    total = jnp.zeros((4 * GROUPS, QUARTER), jnp.float32)
    for head in range(HEADS):
        block = keys_ref[:, pl.ds(head * KEYS_DEV, KEYS_DEV), :].reshape(QUARTER, HALF)
        found = dot(asked, block, NT)
        total = jnp.where(iota((4 * GROUPS, QUARTER), 0) % HEADS == head, found, total)
    for side, ref in enumerate((out_0, out_1, out_2, out_3)):
        ref[...] = total[side * GROUPS : (side + 1) * GROUPS]


def weigh_kernel(
    part_0, part_1, part_2, part_3, second_ref, place_ref, rows_ref, lane_ref, owner_ref, out_ref, weighed
):
    for group in range(GROUPS):
        here = pl.ds(group * TOPK, TOPK)
        place = place_ref[here, :]
        line = pl.ds(group, 1)
        lines = [ref[line, :] for ref in (part_0, part_1, part_2, part_3)]
        score = second_ref[here, :] + picked(jnp.concatenate(lines, axis=1), place)
        raised = jnp.exp(score - jnp.max(score, axis=0, keepdims=True))
        weight = raised / jnp.sum(raised, axis=0, keepdims=True)
        hit = iota((TOPK, LANES), 1) == lane_ref[here, :]
        weighed[here, :] = jnp.where(hit, weight, 0.0).astype(jnp.bfloat16) + rows_ref[0, here, :]
    owner = owner_ref[...]
    total = dot(owner, weighed[...], NN) + dot(owner, rows_ref[1], NN)
    out_ref[:, 0, :] = total


def fetch_kernel(
    here_ref, mail_ref, values_ref, given_ref, kept_ref, row_words, row_spots, tiles, mixes, spot_sem, sems
):
    blocks = 8
    core = here_ref[0]
    mail = jnp.concatenate(
        [mail_ref[pl.ds((1 - core) * CHIPS, CHIPS), 0, :], mail_ref[pl.ds(core * CHIPS, CHIPS), 0, :]], axis=0
    )
    marks = mail.astype(jnp.int32)
    spare = iota((DEVICES, LANES), 0) * (CAP * TILE) + (iota((DEVICES, LANES), 1) & (CAP - 1)) * TILE
    rows = jnp.where(marks > 0, marks - 1, spare)
    row_words[...] = (rows - (rows & (TILE - 1))).T[ROW_LANE : ROW_LANE + CAP, :]
    spots = pltpu.make_async_copy(row_words, row_spots, spot_sem)
    spots.start()
    spots.wait()
    chips_block = DEVICES // blocks

    def issue(block):
        for chip in range(block * chips_block, (block + 1) * chips_block):
            for slot in range(CAP):
                base = pl.multiple_of(row_spots[slot, chip], TILE)
                spot = (chip * CAP + slot) * TILE
                pltpu.make_async_copy(
                    values_ref.at[pl.ds(base, TILE)], tiles.at[pl.ds(spot, TILE)], sems.at[block]
                ).start()

    for block in range(AHEAD):
        issue(block)
    octet = iota((DEVICES, LANES), 1) >> 3
    kept = jnp.where(octet == ROW_LANE >> 3, (rows & (TILE - 1)).astype(jnp.float32), mail)
    kept = jnp.where(octet > ROW_LANE >> 3, 0.0, kept).astype(jnp.bfloat16)
    tall = (8 * DEVICES, LANES)
    spread = jnp.where(iota(tall, 0) >> 3 == iota(tall, 1), 1.0, 0.0).astype(jnp.bfloat16)
    wide = dot(spread, kept, NN)
    octet = iota(tall, 1) >> 3
    weights = jnp.where(octet == iota(tall, 0) & 3, wide, 0.0).astype(jnp.bfloat16)
    within = jnp.where(octet == ROW_LANE >> 3, wide, 0.0).astype(jnp.bfloat16)
    square = (LANES, LANES)
    expand = jnp.where(iota(square, 0) & (CAP - 1) == (iota(square, 1) >> 3) & (CAP - 1), 1.0, 0.0)
    expand = expand.astype(jnp.bfloat16)
    weights = dot(weights, expand, NN)
    within = dot(within, expand, NN).astype(jnp.int32)
    wanted = (within == iota(tall, 1) & (TILE - 1)) & (iota(tall, 1) >> 6 == (iota(tall, 0) >> 3) & 1)
    mixes[...] = jnp.where(wanted, weights, 0.0).astype(jnp.bfloat16)
    upper = iota((32, DV // 2), 0) & 4 == 0
    lower = iota((32, LANES), 0) < 16
    rows_block = chips_block * CAP * TILE
    none = jnp.zeros((32, LANES), jnp.bfloat16)
    for block in range(blocks):
        there = pl.ds(block * rows_block, rows_block)
        pltpu.make_async_copy(values_ref.at[pl.ds(0, rows_block)], tiles.at[there], sems.at[block]).wait()
        if block + AHEAD < blocks:
            issue(block + AHEAD)
        for quad in range(block * chips_block // 4, (block + 1) * chips_block // 4):
            mix = mixes[pl.ds(quad * 32, 32), :]
            mix = jnp.concatenate([jnp.where(lower, mix, none), jnp.where(lower, none, mix)], axis=1)
            total = dot(mix, tiles[pl.ds(quad * 256, 256), :], NN)
            total = jnp.where(upper, total[:, : DV // 2], total[:, DV // 2 :])
            if quad < CHIPS // 4:
                given_ref[pl.ds(quad * 32, 32), :] = total.astype(given_ref.dtype)
            else:
                kept_ref[pl.ds((quad - CHIPS // 4) * 32, 32), :] = total


def finish_kernel(parts_ref, out_ref):
    total = jnp.zeros((8, DV // 2), jnp.float32)
    for chip in range(CHIPS):
        total = total + parts_ref[chip].astype(jnp.float32)
    out_ref[:, : DV // 2] = total[:4].astype(jnp.bfloat16)
    out_ref[:, DV // 2 :] = total[4:].astype(jnp.bfloat16)


VMEM = pl.BlockSpec(memory_space=pltpu.VMEM)
SMEM = pl.BlockSpec(memory_space=pltpu.SMEM)
ANYWHERE = pl.BlockSpec(memory_space=pl.ANY)


def shaped(shape, dtype):
    return jax.ShapeDtypeStruct(shape, dtype)


def partial_rows(here, mail, values):
    return pl.pallas_call(
        fetch_kernel,
        out_shape=(
            shaped((8 * CHIPS, DV // 2), jnp.bfloat16),
            shaped((8 * CHIPS, DV // 2), jnp.float32),
        ),
        in_specs=[SMEM, VMEM, ANYWHERE],
        out_specs=(VMEM, VMEM),
        scratch_shapes=[
            pltpu.VMEM((CAP, DEVICES), jnp.int32),
            pltpu.SMEM((CAP, DEVICES), jnp.int32),
            pltpu.VMEM((CAP * DEVICES * TILE, DV), jnp.bfloat16),
            pltpu.VMEM((8 * DEVICES, LANES), jnp.bfloat16),
            pltpu.SemaphoreType.DMA,
            pltpu.SemaphoreType.DMA((8,)),
        ],
        compiler_params=pltpu.CompilerParams(vmem_limit_bytes=50 * MIB),
        cost_estimate=pl.CostEstimate(flops=10**9, bytes_accessed=20 * MIB, transcendentals=0),
        name="fetch",
    )(here, mail, values)


def swapped(x):
    return lax.ppermute(x, "core", [(0, 1), (1, 0)])


def mirrored(x):
    return lax.ppermute(x, ("half", "z"), [(z, 3 - z) for z in range(4)])


def opposed(x):
    return lax.ppermute(x, ("core", "half", "z"), [(i, 7 - i) for i in range(8)])


def memory_read(queries, indices, first_keys, second_keys, values):
    here = jnp.stack([lax.axis_index("core"), lax.axis_index("half")]).astype(jnp.int32)
    keys = pl.pallas_call(
        repeat_kernel,
        out_shape=shaped((KEY_CHIPS, HEADS * KEYS_DEV, HALF), jnp.bfloat16),
        in_specs=[VMEM],
        out_specs=VMEM,
        compiler_params=pltpu.CompilerParams(vmem_limit_bytes=4 * MIB),
        name="repeat",
    )(first_keys.reshape(HEADS * KEYS_DEV, HALF))
    keys = exchange(keys, KEY_AXES)
    asked = queries.reshape(GROUPS, 2 * HALF)
    asked_first = asked[:, :HALF]
    asked_all = (asked_first, swapped(asked_first), mirrored(asked_first), opposed(asked_first))

    plan = pl.pallas_call(
        plan_kernel,
        out_shape=(
            shaped((ENTRIES, LANES), jnp.float32),
            shaped((ENTRIES, LANES), jnp.int32),
            shaped((2, ENTRIES, LANES), jnp.bfloat16),
            shaped((ENTRIES, LANES), jnp.int32),
            shaped((DEVICES, ENTRIES), jnp.bfloat16),
        ),
        in_specs=[SMEM, VMEM, VMEM, ANYWHERE],
        out_specs=(VMEM,) * 5,
        scratch_shapes=[
            pltpu.VMEM((HEADS, GROUPS, SUBS), jnp.float32),
            pltpu.VMEM((HEADS * SUBS, HALF), jnp.bfloat16),
            pltpu.SemaphoreType.DMA,
        ],
        cost_estimate=pl.CostEstimate(flops=2 * 10**9, bytes_accessed=3 * 1024 * 1024, transcendentals=0),
        compiler_params=pltpu.CompilerParams(vmem_limit_bytes=12 * MIB),
        name="plan",
    )(
        here,
        indices,
        asked[:, HALF:],
        pltpu.with_memory_space_constraint(second_keys.reshape(HEADS * SUBS, HALF), pltpu.HBM),
    )
    second, place, rows, lane, owner = plan

    found = pl.pallas_call(
        match_kernel,
        out_shape=(shaped((GROUPS, QUARTER), jnp.float32),) * 4,
        in_specs=[VMEM] * 5,
        out_specs=(VMEM,) * 4,
        compiler_params=pltpu.CompilerParams(vmem_limit_bytes=8 * MIB),
        name="match",
    )(*asked_all, keys)
    found = (found[0], swapped(found[1]), mirrored(found[2]), opposed(found[3]))
    mail = pl.pallas_call(
        weigh_kernel,
        out_shape=shaped((DEVICES, 1, LANES), jnp.float32),
        in_specs=[VMEM] * 9,
        out_specs=VMEM,
        scratch_shapes=[pltpu.VMEM((ENTRIES, LANES), jnp.bfloat16)],
        compiler_params=pltpu.CompilerParams(vmem_limit_bytes=8 * MIB),
        name="weigh",
    )(*found, second, place, rows, lane, owner)
    mail = exchange(mail, OWNER_AXES)

    given, kept = partial_rows(here, mail, values)
    both = (kept + swapped(given).astype(jnp.float32)).astype(jnp.bfloat16)
    parts = exchange(both.reshape(CHIPS, 8, DV // 2), CHIP_AXES)
    return pl.pallas_call(
        finish_kernel,
        out_shape=shaped((SEQS, DV), jnp.bfloat16),
        in_specs=[VMEM],
        out_specs=VMEM,
        compiler_params=pltpu.CompilerParams(vmem_limit_bytes=8 * MIB),
        name="finish",
    )(parts)


def solution(mesh):
    chips = Mesh(mesh.devices.reshape(4, 4, 2, 2, 2), DEVICE_AXES)
    return jax.shard_map(
        memory_read,
        mesh=chips,
        in_specs=(
            P(DEVICE_AXES, None, None),
            P(DEVICE_AXES, None, None),
            P(None, DEVICE_AXES, None),
            P(),
            P(DEVICE_AXES, None),
        ),
        out_specs=P(DEVICE_AXES, None),
        check_vma=False,
    )
```

time: 83.1 us -> 76.9 us (0.925)
  waiting for transfers between devices: 22.4 us -> 6.41 us
  blocking collectives: 17.1 us -> 31 us
  local copies, waits for them, and re-layouts: 5.88 us -> 2.15 us
    all_to_all x2 -> x1, waiting for transfers between devices: 22.4 us -> 1.42 us  [exchange(): return lax.all_to_all(slots, axes, split_axis=0, concat_axis=0, tiled=True)]
    all_to_all x1 -> x2, blocking collectives: 17.1 us -> 31 us  [exchange(): return lax.all_to_all(slots, axes, split_axis=0, concat_axis=0, tiled=True)]
    ppermute x0 -> x4, starting transfers between devices: none -> 7.48 us  [the longest x2 5.02 us: opposed(): lax.ppermute(x, ('core', 'half', 'z'), [(i, 7 - i) for i in range(8)])]
    all_to_all x2 -> x1, starting transfers between devices: 15.4 us -> 9.21 us  [exchange(): return lax.all_to_all(slots, axes, split_axis=0, concat_axis=0, tiled=True)]
    ppermute x0 -> x4, waiting for transfers between devices: none -> 3.45 us  [the longest x2 2.38 us: mirrored(): return lax.ppermute(x, ('half', 'z'), [(z, 3 - z) for z in range(4)])]
    pallas_call x3, Pallas kernels: 12.3 us -> 9.92 us  [the longest x1 8.79 us: partial_rows(): pl.pallas_call(fetch_kernel, out_shape=(shaped((8 * CHIPS, DV // 2), jnp....]
    pallas_call x1, Pallas kernels: 2.06 us -> 4.26 us  [memory_read(): pl.pallas_call(plan_kernel, out_shape=(shaped((ENTRIES, LANES), jnp.float...]
    broadcast_in_dim x1 -> x0, local copies, waits for them, and re-layouts: 1.82 us -> none  [memory_read(): jnp.broadcast_to(first_keys.reshape(1, HEADS * KEYS_DEV, HALF), (CHIPS, H...]
  transfers between devices with their start and end apart: 5 -> 8, of which waited for: 2 -> 4; matrix products, arithmetic and copies ran while one was open for 3% -> 1% of each run, Pallas kernels for 10% -> 6%
where the time goes in v2:
time: 76.9 us; the launch traced here: 75.7 us
  blocking collectives  31 us (40%)
  starting transfers between devices  20.4 us (27%)
  Pallas kernels  15.4 us (20%)
  waiting for transfers between devices  6.41 us (8%)
  local copies, waits for them, and re-layouts  2.15 us (3%)
    all_to_all x2, blocking collectives, exchange(): return lax.all_to_all(slots, axes, split_axis=0, concat_axis=0, tiled=True)  31 us
    all_to_all x1, starting transfers between devices, exchange(): return lax.all_to_all(slots, axes, split_axis=0, concat_axis=0, tiled=True)  9.21 us
    pallas_call x1, Pallas kernels, partial_rows(): pl.pallas_call(fetch_kernel, out_shape=(shaped((8 * CHIPS, DV // 2), jnp....  8.79 us
    ppermute x2, starting transfers between devices, opposed(): lax.ppermute(x, ('core', 'half', 'z'), [(i, 7 - i) for i in range(8)])  5.02 us
    pallas_call x1, Pallas kernels, memory_read(): pl.pallas_call(plan_kernel, out_shape=(shaped((ENTRIES, LANES), jnp.float...  4.26 us
    ppermute x3, starting transfers between devices, swapped(): return lax.ppermute(x, 'core', [(0, 1), (1, 0)])  3.66 us
    ppermute x2, starting transfers between devices, mirrored(): return lax.ppermute(x, ('half', 'z'), [(z, 3 - z) for z in range(4)])  2.46 us
    ppermute x2, waiting for transfers between devices, mirrored(): return lax.ppermute(x, ('half', 'z'), [(z, 3 - z) for z in range(4)])  2.38 us
  transfers between devices with their start and end apart: 8, of which 4 were waited for; matrix products, arithmetic and copies ran while one was open for 1% of the time, Pallas kernels for 6%

profile of v2, /device:TPU:1, one launch (start us, length us, event | category | flops | bytes accessed | tf_op | source)
XLA Modules:
  0.0 75.7 jit_solution(7648147476122590040)
XLA Ops:
  0.0 0.0 copy-start
  0.0 0.7 copy-done
  0.7 0.9 %repeat.1 = bf16[32,32,256]{2,1,0:T(8,128)(2,1)} custom-call(bf16[32,256]{1,0:T(8,128)(2,1)S(1)} %bitcast.6), custom_call_target="tpu_custom_call" | custom-call | tf_op jit(solution)/shard_map/repeat/pallas_call | solution.py:271
  1.6 9.2 %all-to-all-start = ((bf16[32,32,256]{2,1,0:T(8,128)(2,1)}), bf16[32,32,256]{2,1,0:T(8,128)(2,1)S(1)}, u32[]{:S(2)}, u32[]{:S(2)}) async-start(bf16[32,32,256]{2,1,0:T(8,128)(2,1)} %repeat.1), calls=%async_computation | async-start | bytes 1048576 | tf_op jit(solution)/shard_map/all_to_all | solution.py:46
  10.8 0.7 reshape.12
  11.5 4.5 %collective-permute-start.2 = (bf16[16,256]{1,0:T(8,128)(2,1)S(1)}, bf16[16,256]{1,0:T(8,128)(2,1)S(1)}, u32[]{:S(2)}, u32[]{:S(2)}) collective-permute-start(bf16[16,256]{1,0:T(8,128)(2,1)S(1)} %get-tuple-element.28.asked_0), channel_id=1, source_target_pairs={{0,7},{1,6},{2,5},{3,4},{4,3},{5,2},{6,1},{7,0},{8,15},{9,14},{10,... | collective-permute-start | bytes 24584 | tf_op jit(solution)/shard_map/ppermute | solution.py:266
  16.1 0.0 collective-permute-start.1
  16.1 0.5 collective-permute-start
  16.6 0.1 pad_add_fusion.here_ref
  16.6 1.1 %collective-permute-done.2.asked_3 = bf16[16,256]{1,0:T(8,128)(2,1)S(1)} collective-permute-done((bf16[16,256]{1,0:T(8,128)(2,1)S(1)}, bf16[16,256]{1,0:T(8,128)(2,1)S(1)}, u32[]{:S(2)}, u32[]{:S(2)}) %collective-permute-start.2) | collective-permute-done | bytes 8224 | tf_op jit(solution)/shard_map/ppermute | solution.py:266
  17.7 2.4 %collective-permute-done.1.asked_2 = bf16[16,256]{1,0:T(8,128)(2,1)S(1)} collective-permute-done((bf16[16,256]{1,0:T(8,128)(2,1)S(1)}, bf16[16,256]{1,0:T(8,128)(2,1)S(1)}, u32[]{:S(2)}, u32[]{:S(2)}) %collective-permute-start.1) | collective-permute-done | bytes 8224 | tf_op jit(solution)/shard_map/ppermute | solution.py:262
  20.1 0.0 collective-permute-done.asked_1
  20.1 1.4 %all-to-all-done.keys_ref = bf16[32,32,256]{2,1,0:T(8,128)(2,1)S(1)} async-done(((bf16[32,32,256]{2,1,0:T(8,128)(2,1)}), bf16[32,32,256]{2,1,0:T(8,128)(2,1)S(1)}, u32[]{:S(2)}, u32[]{:S(2)}) %all-to-all-start) | async-done | bytes 524320 | tf_op jit(solution)/shard_map/all_to_all | solution.py:46
  21.5 0.3 match.1
  21.8 2.4 %collective-permute-start.3 = (f32[16,256]{1,0:T(8,128)S(1)}, f32[16,256]{1,0:T(8,128)S(1)}, u32[]{:S(2)}, u32[]{:S(2)}) collective-permute-start(f32[16,256]{1,0:T(8,128)S(1)} %get-tuple-element.17), channel_id=1, source_target_pairs={{0,4},{4,0},{1,5},{5,1},{2,6},{6,2},{3,7},{7,3},{8,12},{12,8},{9,1... | collective-permute-start | bytes 49160 | tf_op jit(solution)/shard_map/ppermute | solution.py:258
  24.2 2.5 %collective-permute-start.4 = (f32[16,256]{1,0:T(8,128)S(1)}, f32[16,256]{1,0:T(8,128)S(1)}, u32[]{:S(2)}, u32[]{:S(2)}) collective-permute-start(f32[16,256]{1,0:T(8,128)S(1)} %get-tuple-element.18), channel_id=1, source_target_pairs={{0,3},{1,2},{2,1},{3,0},{4,7},{5,6},{6,5},{7,4},{8,11},{9,10},{10,... | collective-permute-start | bytes 49160 | tf_op jit(solution)/shard_map/ppermute | solution.py:262
  26.6 0.5 collective-permute-start.5
  27.1 0.0 copy-start.1
  27.1 0.7 copy-done.1
  27.8 4.3 %plan.1 = (f32[512,128]{1,0:T(8,128)S(1)}, s32[512,128]{1,0:T(8,128)S(1)}, bf16[2,512,128]{2,1,0:T(8,128)(2,1)S(1)}, s32[512,128]{1,0:T(8,128)S(1)}, bf16[128,512]{1,0:T(8,128)(2,1)S(1)}) custom-call(s32[2]{0:T(128)S(1)} %pad_add_fusion.here_ref, s32[4,4,32]{2,1,0:T(4,128)S(1)} %copy-done.1, bf16[16,256]{1,0:T(8,128)(2,1)S(1)} %get-tuple-element.27.query_ref, ...), custom_call_target="tpu_custom_call" | custom-call | flops 2000000000 | bytes 3145728 | tf_op jit(solution)/shard_map/plan/pallas_call | solution.py:284
  32.1 0.0 collective-permute-done.3.part_1
  32.1 0.0 collective-permute-done.4.part_2
  32.1 0.0 collective-permute-done.5.part_3
  32.1 0.5 weigh.1
  32.6 14.3 %all_to_all.15.mail_ref = f32[128,1,128]{2,1,0:T(1,128)S(1)} all-to-all(f32[128,1,128]{2,1,0:T(1,128)S(1)} %weigh.1), channel_id=1, replica_groups=mesh['x'=4,'y'=4,'core'=2,'half'=2,'z'=2] {'core','x','y','half','z'}, dimensions={0} | all-to-all | bytes 131072 | tf_op jit(solution)/shard_map/all_to_all | solution.py:46
  46.9 8.8 %fetch.1 = (bf16[512,512]{1,0:T(8,128)(2,1)S(1)}, f32[512,512]{1,0:T(8,128)S(1)}) custom-call(s32[2]{0:T(128)S(1)} %pad_add_fusion.here_ref, f32[128,1,128]{2,1,0:T(1,128)S(1)} %all_to_all.15.mail_ref, bf16[8192,1024]{1,0:T(8,128)(2,1)} %values_ref.1), custom_call_target="tpu_custom_call" | custom-call | flops 1000000000 | bytes 20971520 | tf_op jit(solution)/shard_map/fetch/pallas_call | solution.py:235
  55.7 0.8 %collective-permute-start.6 = (bf16[512,512]{1,0:T(8,128)(2,1)S(1)}, bf16[512,512]{1,0:T(8,128)(2,1)S(1)}, u32[]{:S(2)}, u32[]{:S(2)}) collective-permute-start(bf16[512,512]{1,0:T(8,128)(2,1)S(1)} %get-tuple-element.26), channel_id=1, source_target_pairs={{0,4},{4,0},{1,5},{5,1},{2,6},{6,2},{3,7},{7,3},{8,12},{12,8},{9,1... | collective-permute-start | bytes 1572872 | tf_op jit(solution)/shard_map/ppermute | solution.py:258
  56.5 1.5 %collective-permute-done.6 = bf16[512,512]{1,0:T(8,128)(2,1)S(1)} collective-permute-done((bf16[512,512]{1,0:T(8,128)(2,1)S(1)}, bf16[512,512]{1,0:T(8,128)(2,1)S(1)}, u32[]{:S(2)}, u32[]{:S(2)}) %collective-permute-start.6) | collective-permute-done | bytes 524320 | tf_op jit(solution)/shard_map/ppermute | solution.py:258
  58.0 0.2 fusion
  58.3 16.8 %all_to_all.16.parts_ref = bf16[64,8,512]{2,1,0:T(8,128)(2,1)S(1)} all-to-all(bf16[64,8,512]{2,1,0:T(8,128)(2,1)S(1)} %fusion), channel_id=1, replica_groups=mesh['x'=4,'y'=4,'core'=2,'half'=2,'z'=2] {'x','y','half','z'}, dimensions={0} | all-to-all | bytes 1048576 | tf_op jit(solution)/shard_map/all_to_all | solution.py:46
  75.0 0.7 finish.1
  (1 shorter events, 0.0 us)
Async XLA Ops:
  0.0 0.7 copy-start
  1.6 19.9 %all-to-all-start = ((bf16[32,32,256]{2,1,0:T(8,128)(2,1)}), bf16[32,32,256]{2,1,0:T(8,128)(2,1)S(1)}, u32[]{:S(2)}, u32[]{:S(2)}) async-start(bf16[32,32,256]{2,1,0:T(8,128)(2,1)} %repeat.1), calls=%async_computation | async-start | bytes 1048576 | tf_op jit(solution)/shard_map/all_to_all | solution.py:46
  11.5 6.2 %collective-permute-start.2 = (bf16[16,256]{1,0:T(8,128)(2,1)S(1)}, bf16[16,256]{1,0:T(8,128)(2,1)S(1)}, u32[]{:S(2)}, u32[]{:S(2)}) collective-permute-start(bf16[16,256]{1,0:T(8,128)(2,1)S(1)} %get-tuple-element.28.asked_0), channel_id=1, source_target_pairs={{0,7},{1,6},{2,5},{3,4},{4,3},{5,2},{6,1},{7,0},{8,15},{9,14},{10,... | collective-permute-start | bytes 24584 | tf_op jit(solution)/shard_map/ppermute | solution.py:266
  16.1 4.0 %collective-permute-start.1 = (bf16[16,256]{1,0:T(8,128)(2,1)S(1)}, bf16[16,256]{1,0:T(8,128)(2,1)S(1)}, u32[]{:S(2)}, u32[]{:S(2)}) collective-permute-start(bf16[16,256]{1,0:T(8,128)(2,1)S(1)} %get-tuple-element.28.asked_0), channel_id=1, source_target_pairs={{0,3},{1,2},{2,1},{3,0},{4,7},{5,6},{6,5},{7,4},{8,11},{9,10},{10,... | collective-permute-start | bytes 24584 | tf_op jit(solution)/shard_map/ppermute | solution.py:262
  16.1 4.0 %collective-permute-start = (bf16[16,256]{1,0:T(8,128)(2,1)S(1)}, bf16[16,256]{1,0:T(8,128)(2,1)S(1)}, u32[]{:S(2)}, u32[]{:S(2)}) collective-permute-start(bf16[16,256]{1,0:T(8,128)(2,1)S(1)} %get-tuple-element.28.asked_0), channel_id=1, source_target_pairs={{0,4},{4,0},{1,5},{5,1},{2,6},{6,2},{3,7},{7,3},{8,12},{12,8},{9,1... | collective-permute-start | bytes 24584 | tf_op jit(solution)/shard_map/ppermute | solution.py:258
  21.8 10.3 %collective-permute-start.3 = (f32[16,256]{1,0:T(8,128)S(1)}, f32[16,256]{1,0:T(8,128)S(1)}, u32[]{:S(2)}, u32[]{:S(2)}) collective-permute-start(f32[16,256]{1,0:T(8,128)S(1)} %get-tuple-element.17), channel_id=1, source_target_pairs={{0,4},{4,0},{1,5},{5,1},{2,6},{6,2},{3,7},{7,3},{8,12},{12,8},{9,1... | collective-permute-start | bytes 49160 | tf_op jit(solution)/shard_map/ppermute | solution.py:258
  24.2 7.9 %collective-permute-start.4 = (f32[16,256]{1,0:T(8,128)S(1)}, f32[16,256]{1,0:T(8,128)S(1)}, u32[]{:S(2)}, u32[]{:S(2)}) collective-permute-start(f32[16,256]{1,0:T(8,128)S(1)} %get-tuple-element.18), channel_id=1, source_target_pairs={{0,3},{1,2},{2,1},{3,0},{4,7},{5,6},{6,5},{7,4},{8,11},{9,10},{10,... | collective-permute-start | bytes 49160 | tf_op jit(solution)/shard_map/ppermute | solution.py:262
  26.6 5.5 %collective-permute-start.5 = (f32[16,256]{1,0:T(8,128)S(1)}, f32[16,256]{1,0:T(8,128)S(1)}, u32[]{:S(2)}, u32[]{:S(2)}) collective-permute-start(f32[16,256]{1,0:T(8,128)S(1)} %get-tuple-element.19), channel_id=1, source_target_pairs={{0,7},{1,6},{2,5},{3,4},{4,3},{5,2},{6,1},{7,0},{8,15},{9,14},{10,... | collective-permute-start | bytes 49160 | tf_op jit(solution)/shard_map/ppermute | solution.py:266
  27.1 0.7 copy-start.1
  55.7 2.3 %collective-permute-start.6 = (bf16[512,512]{1,0:T(8,128)(2,1)S(1)}, bf16[512,512]{1,0:T(8,128)(2,1)S(1)}, u32[]{:S(2)}, u32[]{:S(2)}) collective-permute-start(bf16[512,512]{1,0:T(8,128)(2,1)S(1)} %get-tuple-element.26), channel_id=1, source_target_pairs={{0,4},{4,0},{1,5},{5,1},{2,6},{6,2},{3,7},{7,3},{8,12},{12,8},{9,1... | collective-permute-start | bytes 1572872 | tf_op jit(solution)/shard_map/ppermute | solution.py:258
